TPU v7x, 32 devices: a whole 2x2x4 slice. The times are simulated.
32 devices in a mesh: snap: 8 (over z, x), bin: 4 (over y, core).
Axes of the slice: x: 2, y: 2, z: 4, core: 2. Of those that a mesh axis runs over, the one named last changes fastest.
Arguments:
- data: bfloat16 [256, 128, 1024], P(None, ('snap', 'bin')), may hold values from -6 to 6
- steering: bfloat16 [256, 1024, 2048], P(('snap', 'bin')), may hold values from -2 to 2
- start: float32 [256, 1024, 64], P(('snap', 'bin')), may hold values from -6 to 6
Outputs:
- projector: float32 [256, 1024, 1024], P(('snap', 'bin'))
- spectrum: float32 [2048], replicated
All inputs are finite; a program needn't handle non-finite values.
Results may differ from a plain program's by a relative error of at most 0.00042.
Values may be sent and summed in bfloat16 or wider, within the bound.
A program may use at most 128 MiB of HBM per device.

v0:
```python
import functools

import jax
import jax.numpy as jnp
from jax import lax
from jax.experimental import pallas as pl
from jax.experimental.pallas import tpu as pltpu

ITERS = 3
F32 = jnp.float32
BF16 = jnp.bfloat16
MESH = pl.DeviceIdType.MESH
VMEM_LIMIT = 64000 * 1024


def place(d, inner):
    return (d // inner, lax.rem(d, inner))


def greet_all(me, n, inner):
    barrier = pltpu.get_barrier_semaphore()

    def one(o, c):
        pl.semaphore_signal(
            barrier, inc=1, device_id=place(lax.rem(me + o, n), inner), device_id_type=MESH
        )
        return c

    lax.fori_loop(1, n, one, 0)
    pl.semaphore_wait(barrier, n - 1)


def exchange_kernel(n, inner, nb, data_ref, out_ref, send_sem, recv_sem, own_sem):
    me = lax.axis_index("snap") * inner + lax.axis_index("bin")
    own = pltpu.make_async_copy(data_ref.at[pl.ds(me * nb, nb)], out_ref.at[:, 0], own_sem)
    own.start()
    greet_all(me, n, inner)

    def copy(o):
        d = lax.rem(me + o, n)
        return pltpu.make_async_remote_copy(
            src_ref=data_ref.at[pl.ds(d * nb, nb)],
            dst_ref=out_ref.at[:, o],
            send_sem=send_sem.at[o],
            recv_sem=recv_sem.at[o],
            device_id=place(d, inner),
            device_id_type=MESH,
        )

    def start(o, c):
        copy(o).start()
        return c

    def finish(o, c):
        copy(o).wait()
        return c

    lax.fori_loop(1, n, start, 0)
    own.wait()
    lax.fori_loop(1, n, finish, 0)


def exchange(data, n, inner):
    bins, rows, width = data.shape
    nb = bins // n
    return pl.pallas_call(
        functools.partial(exchange_kernel, n, inner, nb),
        out_shape=jax.ShapeDtypeStruct((nb, n, rows, width), data.dtype),
        in_specs=[pl.BlockSpec(memory_space=pl.ANY)],
        out_specs=pl.BlockSpec(memory_space=pl.ANY),
        scratch_shapes=[
            pltpu.SemaphoreType.DMA((n,)),
            pltpu.SemaphoreType.DMA((n,)),
            pltpu.SemaphoreType.DMA,
        ],
        compiler_params=pltpu.CompilerParams(collective_id=0, has_side_effects=True),
        name="exchange",
    )(data)


def total_kernel(n, inner, scale, noise_ref, out_ref, held, send_sem, recv_sem):
    me = lax.axis_index("snap") * inner + lax.axis_index("bin")
    held[pl.ds(me, 1)] = noise_ref[...]
    greet_all(me, n, inner)

    def copy(o, slot):
        return pltpu.make_async_remote_copy(
            src_ref=noise_ref.at[0],
            dst_ref=held.at[slot],
            send_sem=send_sem.at[o],
            recv_sem=recv_sem.at[o],
            device_id=place(lax.rem(me + o, n), inner),
            device_id_type=MESH,
        )

    def start(o, c):
        copy(o, me).start()
        return c

    def finish(o, c):
        copy(o, lax.rem(me - o + n, n)).wait()
        return c

    lax.fori_loop(1, n, start, 0)
    lax.fori_loop(1, n, finish, 0)
    out_ref[...] = scale / jnp.sum(held[...], axis=0)


def total(noise, n, inner, scale):
    rows, width = noise.shape[1:]
    return pl.pallas_call(
        functools.partial(total_kernel, n, inner, scale),
        out_shape=jax.ShapeDtypeStruct((rows, width), F32),
        in_specs=[pl.BlockSpec(memory_space=pltpu.VMEM)],
        out_specs=pl.BlockSpec(memory_space=pltpu.VMEM),
        scratch_shapes=[
            pltpu.VMEM((n, rows, width), F32),
            pltpu.SemaphoreType.DMA((n,)),
            pltpu.SemaphoreType.DMA((n,)),
        ],
        compiler_params=pltpu.CompilerParams(collective_id=1, has_side_effects=True),
        name="total",
    )(noise)


def split(a):
    high = a.astype(BF16).astype(F32)
    rest = a - high
    mid = rest.astype(BF16).astype(F32)
    return high, mid, rest - mid


def stack(parts, axis):
    return jnp.concatenate(parts, axis=axis).astype(BF16)


def dot(a, b, ca, cb):
    return lax.dot_general(a, b, (((ca,), (cb,)), ((), ())), preferred_element_type=F32)


def fold_rows(p):
    r = p.shape[0] // 3
    return p[:r] + (p[r : 2 * r] + p[2 * r :])


def fold_lanes(p):
    c = p.shape[1] // 3
    return p[:, :c] + (p[:, c : 2 * c] + p[:, 2 * c :])


def inverse_factors(grams):
    size = grams[0].shape[0]
    eye = (
        lax.broadcasted_iota(jnp.int32, (size, size), 0)
        == lax.broadcasted_iota(jnp.int32, (size, size), 1)
    ).astype(F32)
    rest = [jnp.concatenate([g, eye], axis=1) for g in grams]
    wide = 2 * size
    sub = lax.broadcasted_iota(jnp.int32, (8, wide), 0)
    lane = lax.broadcasted_iota(jnp.int32, (8, size), 1)
    done = [[] for _ in grams]
    for t in range(size // 8):
        tiles = [a[8 * t : 8 * t + 8] for a in rest]
        cols = [
            [jnp.broadcast_to(a[:, 8 * t + j : 8 * t + j + 1], (8, wide)) for j in range(8)]
            for a in tiles
        ]
        invs = [jnp.zeros((8, wide), F32) for _ in tiles]
        for j in range(8):
            for i in range(len(tiles)):
                c = cols[i]
                inv = 1.0 / c[j][j : j + 1]
                below = jnp.where(sub > j, c[j], 0.0)
                tiles[i] = tiles[i] - below * (tiles[i][j : j + 1] * inv)
                for k in range(j + 1, 8):
                    c[k] = c[k] - below * (c[k][j : j + 1] * inv)
                invs[i] = jnp.where(sub == j, inv, invs[i])
        for i in range(len(tiles)):
            done[i].append(tiles[i] * jnp.sqrt(invs[i]))
            if 8 * t + 8 < size:
                scaled = (tiles[i] * invs[i])[:, :size]
                h, m, l = split(jnp.where(lane >= 8 * t + 8, scaled, 0.0))
                rh, rm, rl = split(tiles[i])
                rest[i] = rest[i] - dot(
                    stack([l, h, m, m, h, h], 0), stack([rh, rl, rm, rh, rm, rh], 0), 0, 0
                )
    return [jnp.concatenate(d, axis=0)[:, size:] for d in done]


def music_kernel(
    x_ref, start_ref, steer_ref, proj_ref, noise_ref, steer_v, out_v, x_v, s_v, v_v, in_sem, out_sem
):
    nb, n, rows, m = x_ref.shape
    kk = n * rows
    g = steer_ref.shape[2]

    def load(b):
        return pltpu.make_async_copy(steer_ref.at[b], steer_v.at[b], in_sem.at[b])

    def put(b, slot):
        return pltpu.make_async_copy(out_v.at[slot], proj_ref.at[b], out_sem.at[slot])

    for b in range(nb):
        load(b).start()

    def prepare(b, c):
        x = x_ref[b].reshape(kk, m)
        x_v[b] = x
        s_v[b] = stack(split(dot(x, x, 1, 1)), 1)
        v_v[b] = fold_rows(dot(stack(split(start_ref[b]), 0), x, 1, 1))
        return c

    lax.fori_loop(0, nb, prepare, 0)

    def step(it, c):
        last = it == ITERS - 1
        kept, grams = [], []
        for b in range(nb):
            v = v_v[b]
            vs = stack(split(v), 0)
            w = fold_rows(fold_lanes(dot(vs, s_v[b], 1, 0)))
            grams.append(fold_lanes(fold_rows(dot(stack(split(w), 0), vs, 1, 1))))
            kept.append(jnp.where(last, v, w * (1.0 / kk)))
        for b, factor in enumerate(inverse_factors(grams)):
            p = dot(stack(split(factor), 0), stack(split(kept[b]), 1), 1, 0)
            v_v[b] = fold_rows(fold_lanes(p))
        return c

    lax.fori_loop(0, ITERS, step, 0)
    noise_ref[...] = jnp.zeros_like(noise_ref)

    def finish(b, c):
        slot = lax.rem(b, 2)
        basis = fold_rows(dot(stack(split(v_v[b]), 0), x_v[b], 1, 0))
        low = basis.astype(BF16)
        wide = low.astype(F32)
        tail = basis - wide
        left = stack([wide, tail, wide], 0)
        right = stack([wide, wide, tail], 0)

        @pl.when(b >= 2)
        def _():
            put(b - 2, slot).wait()

        step_rows = m // 4
        for r in range(0, m, step_rows):
            out_v[slot, r : r + step_rows] = dot(left[:, r : r + step_rows], right, 0, 0)
        put(b, slot).start()
        load(b).wait()
        step_lanes = g // 4
        for q in range(0, g, step_lanes):
            along = dot(low, steer_v[b, :, q : q + step_lanes], 1, 0)
            energy = jnp.zeros((8, step_lanes), F32)
            for r in range(0, m, 64):
                part = steer_v[b, r : r + 64, q : q + step_lanes].astype(F32)
                energy = energy + jnp.sum((part * part).reshape(8, 8, step_lanes), axis=0)
            noise_ref[0, :, q : q + step_lanes] += jnp.sum(energy, axis=0, keepdims=True) - jnp.sum(
                along * along, axis=0, keepdims=True
            )
        return c

    lax.fori_loop(0, nb, finish, 0)
    for b in range(max(nb - 2, 0), nb):
        put(b, b % 2).wait()


def music(x, start, steering):
    nb, n, rows, m = x.shape
    kk = n * rows
    width = start.shape[1]
    g = steering.shape[2]
    return pl.pallas_call(
        music_kernel,
        out_shape=(
            jax.ShapeDtypeStruct((nb, m, m), F32),
            jax.ShapeDtypeStruct((1, 1, g), F32),
        ),
        in_specs=[
            pl.BlockSpec(memory_space=pltpu.VMEM),
            pl.BlockSpec(memory_space=pltpu.VMEM),
            pl.BlockSpec(memory_space=pl.ANY),
        ],
        out_specs=(
            pl.BlockSpec(memory_space=pl.ANY),
            pl.BlockSpec(memory_space=pltpu.VMEM),
        ),
        scratch_shapes=[
            pltpu.VMEM((nb, m, g), BF16),
            pltpu.VMEM((2, m, m), F32),
            pltpu.VMEM((nb, kk, m), BF16),
            pltpu.VMEM((nb, kk, 3 * kk), BF16),
            pltpu.VMEM((nb, width, kk), F32),
            pltpu.SemaphoreType.DMA((nb,)),
            pltpu.SemaphoreType.DMA((2,)),
        ],
        compiler_params=pltpu.CompilerParams(vmem_limit_bytes=VMEM_LIMIT),
        name="music",
    )(x, start, steering)


def on_device(n, inner, data, steering, start):
    bins, rows, m = data.shape
    owned = exchange(data, n, inner)
    projector, noise = music(owned, start.transpose(0, 2, 1), steering)
    spectrum = total(noise, n, inner, float(bins * m))
    return (projector, spectrum.reshape(-1))


def solution(mesh):
    P = jax.sharding.PartitionSpec
    inner = mesh.shape["bin"]
    n = mesh.shape["snap"] * inner
    both = ("snap", "bin")
    return jax.shard_map(
        functools.partial(on_device, n, inner),
        mesh=mesh,
        in_specs=(P(None, both, None), P(both, None, None), P(both, None, None)),
        out_specs=(P(both, None, None), P()),
        check_vma=False,
    )
```

profile of v0, /device:TPU:0, one launch (start us, length us, event | category | flops | bytes accessed | tf_op | source)
XLA Modules:
  0.0 108.0 jit_solution(16737406624905040587)
XLA Ops:
  0.6 45.0 %exchange.1.x_ref = bf16[8,32,4,1024]{3,2,1,0:T(4,128)(2,1)} custom-call(bf16[256,4,1024]{2,1,0:T(4,128)(2,1)} %data_ref.1), custom_call_target="tpu_custom_call" | custom-call | tf_op jit(solution)/shard_map/exchange/pallas_call | solution.py:66
  45.7 38.0 %music.1 = (f32[8,1024,1024]{2,1,0:T(8,128)}, f32[1,1,2048]{2,1,0:T(1,128)}) custom-call(bf16[8,32,4,1024]{3,2,1,0:T(4,128)(2,1)} %exchange.1.x_ref, f32[8,64,1024]{2,1,0:T(8,128)} %bitcast.2, bf16[8,1024,2048]{2,1,0:T(8,128)(2,1)} %steer_ref.1), custom_call_target="tpu_custom_call" | custom-call | tf_op jit(solution)/shard_map/music/pallas_call | solution.py:272
  83.6 23.1 %total.1 = f32[1,2048]{1,0:T(1,128)} custom-call(f32[1,1,2048]{2,1,0:T(1,128)} %get-tuple-element.5.noise_ref), custom_call_target="tpu_custom_call" | custom-call | tf_op jit(solution)/shard_map/total/pallas_call | solution.py:111
  106.7 1.3 %copy.6 = f32[2048]{0:T(1024)} copy(f32[2048]{0:T(1024)} %bitcast.3) | data formatting | bytes 16384
where the time goes:
time: 108 us
  Pallas kernels  106 us (98%)
  local copies, waits for them, and re-layouts  1.3 us (1%)
    pallas_call x1, Pallas kernels, exchange(): pl.pallas_call(functools.partial(exchange_kernel, n, inner, nb), out_shap...  45 us
    pallas_call x1, Pallas kernels, music(): pl.pallas_call(music_kernel, out_shape=(jax.ShapeDtypeStruct((nb, m, m),...  38 us
    pallas_call x1, Pallas kernels, total(): pl.pallas_call(functools.partial(total_kernel, n, inner, scale), out_shap...  23.1 us

commit v1 on v0

v1 whole, which is shorter than its diff:
```python
import functools

import jax
import jax.numpy as jnp
from jax import lax
from jax.experimental import pallas as pl
from jax.experimental.pallas import tpu as pltpu

ITERS = 3
F32 = jnp.float32
BF16 = jnp.bfloat16
MESH = pl.DeviceIdType.MESH
VMEM_LIMIT = 60 * 1024 * 1024
BOTH = ("snap", "bin")


def place(d, inner):
    return (d // inner, lax.rem(d, inner))


def greet_all(me, n, inner):
    barrier = pltpu.get_barrier_semaphore()

    def one(o, c):
        pl.semaphore_signal(
            barrier, inc=1, device_id=place(lax.rem(me + o, n), inner), device_id_type=MESH
        )
        return c

    lax.fori_loop(1, n, one, 0)
    pl.semaphore_wait(barrier, n - 1)


def split(a):
    high = a.astype(BF16).astype(F32)
    rest = a - high
    mid = rest.astype(BF16).astype(F32)
    return high, mid, rest - mid


def stack(parts, axis):
    return jnp.concatenate(parts, axis=axis).astype(BF16)


def dot(a, b, ca, cb):
    return lax.dot_general(a, b, (((ca,), (cb,)), ((), ())), preferred_element_type=F32)


def fold_rows(p):
    r = p.shape[0] // 3
    return p[:r] + (p[r : 2 * r] + p[2 * r :])


def fold_lanes(p):
    c = p.shape[1] // 3
    return p[:, :c] + (p[:, c : 2 * c] + p[:, 2 * c :])


def inverse_factors(grams):
    size = grams[0].shape[0]
    eye = (
        lax.broadcasted_iota(jnp.int32, (size, size), 0)
        == lax.broadcasted_iota(jnp.int32, (size, size), 1)
    ).astype(F32)
    rest = [jnp.concatenate([g, eye], axis=1) for g in grams]
    wide = 2 * size
    sub = lax.broadcasted_iota(jnp.int32, (8, wide), 0)
    lane = lax.broadcasted_iota(jnp.int32, (8, size), 1)
    done = [[] for _ in grams]
    for t in range(size // 8):
        tiles = [a[8 * t : 8 * t + 8] for a in rest]
        cols = [
            [jnp.broadcast_to(a[:, 8 * t + j : 8 * t + j + 1], (8, wide)) for j in range(8)]
            for a in tiles
        ]
        invs = [jnp.zeros((8, wide), F32) for _ in tiles]
        for j in range(8):
            for i in range(len(tiles)):
                c = cols[i]
                inv = 1.0 / c[j][j : j + 1]
                below = jnp.where(sub > j, c[j], 0.0)
                tiles[i] = tiles[i] - below * (tiles[i][j : j + 1] * inv)
                for k in range(j + 1, 8):
                    c[k] = c[k] - below * (c[k][j : j + 1] * inv)
                invs[i] = jnp.where(sub == j, inv, invs[i])
        for i in range(len(tiles)):
            done[i].append(tiles[i] * jnp.sqrt(invs[i]))
            if 8 * t + 8 < size:
                scaled = (tiles[i] * invs[i])[:, :size]
                h, m, l = split(jnp.where(lane >= 8 * t + 8, scaled, 0.0))
                rh, rm, rl = split(tiles[i])
                rest[i] = rest[i] - dot(
                    stack([l, h, m, m, h, h], 0), stack([rh, rl, rm, rh, rm, rh], 0), 0, 0
                )
    return [jnp.concatenate(d, axis=0)[:, size:] for d in done]


def collect_kernel(
    n, inner, data_ref, start_ref, steer_ref, basis_ref, noise_ref,
    x_v, start_v, steer_v, flat_v, s_v, v_v, basis_v, power_v,
    send_sem, recv_sem, own_sem, start_sem, steer_sem, basis_sem,
):
    nb, _, rows, m = x_v.shape
    kk = n * rows
    g = steer_ref.shape[2]
    group = flat_v.shape[0]
    groups = nb // group
    me = lax.axis_index("snap") * inner + lax.axis_index("bin")

    own = pltpu.make_async_copy(data_ref.at[pl.ds(me * nb, nb)], x_v.at[:, 0], own_sem)
    first = pltpu.make_async_copy(start_ref, start_v, start_sem)

    def load(b):
        return pltpu.make_async_copy(steer_ref.at[b], steer_v.at[b], steer_sem.at[b])

    def put(p):
        return pltpu.make_async_copy(
            basis_v.at[pl.ds(p * group, group)], basis_ref.at[pl.ds(p * group, group)], basis_sem.at[p]
        )

    own.start()
    first.start()

    def fetch(b, c):
        load(b).start()
        return c

    lax.fori_loop(0, nb, fetch, 0)
    greet_all(me, n, inner)

    def copy(p, o):
        d = lax.rem(me + o, n)
        return pltpu.make_async_remote_copy(
            src_ref=data_ref.at[pl.ds(d * nb + p * group, group)],
            dst_ref=x_v.at[pl.ds(p * group, group), o],
            send_sem=send_sem.at[p],
            recv_sem=recv_sem.at[p],
            device_id=place(d, inner),
            device_id_type=MESH,
        )

    def post(p, c):
        def one(o, cc):
            copy(p, o).start()
            return cc

        return lax.fori_loop(1, n, one, c)

    lax.fori_loop(0, groups, post, 0)

    def arrived(p, sem):
        block = x_v.at[pl.ds(p * group, group), pl.ds(1, n - 1)]
        pltpu.make_async_copy(block, block, sem.at[p]).wait()

    power_v[...] = jnp.zeros_like(power_v)
    lanes = g // 4

    def energies(b, c):
        load(b).wait()
        for q in range(0, g, lanes):
            energy = power_v[:, q : q + lanes]
            for r in range(0, m, 64):
                part = steer_v[b, r : r + 64, q : q + lanes].astype(F32)
                energy = energy + jnp.sum((part * part).reshape(8, 8, lanes), axis=0)
            power_v[:, q : q + lanes] = energy
        return c

    lax.fori_loop(0, nb, energies, 0)
    noise_ref[...] = jnp.sum(power_v[...], axis=0, keepdims=True)
    own.wait()
    first.wait()

    def process(p, c):
        arrived(p, recv_sem)
        for i in range(group):
            b = p * group + i
            x = x_v[b].reshape(kk, m)
            flat_v[i] = x
            s_v[i] = stack(split(dot(x, x, 1, 1)), 1)
            v_v[i] = fold_rows(dot(stack(split(start_v[b]), 0), x, 1, 1))

        def step(it, cc):
            last = it == ITERS - 1
            kept, grams = [], []
            for i in range(group):
                v = v_v[i]
                vs = stack(split(v), 0)
                w = fold_rows(fold_lanes(dot(vs, s_v[i], 1, 0)))
                grams.append(fold_lanes(fold_rows(dot(stack(split(w), 0), vs, 1, 1))))
                kept.append(jnp.where(last, v, w * (1.0 / kk)))
            for i, factor in enumerate(inverse_factors(grams)):
                q = dot(stack(split(factor), 0), stack(split(kept[i]), 1), 1, 0)
                v_v[i] = fold_rows(fold_lanes(q))
            return cc

        lax.fori_loop(0, ITERS, step, 0)
        for i in range(group):
            b = p * group + i
            basis = fold_rows(dot(stack(split(v_v[i]), 0), flat_v[i], 1, 0))
            low = basis.astype(BF16)
            basis_v[b, 0] = low
            basis_v[b, 1] = (basis - low.astype(F32)).astype(BF16)
            for q in range(0, g, lanes):
                along = dot(low, steer_v[b, :, q : q + lanes], 1, 0)
                noise_ref[:, q : q + lanes] -= jnp.sum(along * along, axis=0, keepdims=True)
        put(p).start()
        return c

    lax.fori_loop(0, groups, process, 0)

    def close(p, c):
        arrived(p, send_sem)
        put(p).wait()
        return c

    lax.fori_loop(0, groups, close, 0)


def collect(data, start, steering, n, inner):
    bins, rows, m = data.shape
    nb = bins // n
    kk = n * rows
    width = start.shape[1]
    g = steering.shape[2]
    group = 2 if nb % 2 == 0 else 1
    groups = nb // group
    return pl.pallas_call(
        functools.partial(collect_kernel, n, inner),
        out_shape=(
            jax.ShapeDtypeStruct((nb, 2, width, m), BF16),
            jax.ShapeDtypeStruct((1, g), F32),
        ),
        in_specs=[pl.BlockSpec(memory_space=pl.ANY)] * 3,
        out_specs=(
            pl.BlockSpec(memory_space=pl.ANY),
            pl.BlockSpec(memory_space=pltpu.VMEM),
        ),
        scratch_shapes=[
            pltpu.VMEM((nb, n, rows, m), BF16),
            pltpu.VMEM((nb, width, m), F32),
            pltpu.VMEM((nb, m, g), BF16),
            pltpu.VMEM((group, kk, m), BF16),
            pltpu.VMEM((group, kk, 3 * kk), BF16),
            pltpu.VMEM((group, width, kk), F32),
            pltpu.VMEM((nb, 2, width, m), BF16),
            pltpu.VMEM((8, g), F32),
            pltpu.SemaphoreType.DMA((groups,)),
            pltpu.SemaphoreType.DMA((groups,)),
            pltpu.SemaphoreType.DMA,
            pltpu.SemaphoreType.DMA,
            pltpu.SemaphoreType.DMA((nb,)),
            pltpu.SemaphoreType.DMA((groups,)),
        ],
        compiler_params=pltpu.CompilerParams(
            collective_id=0, has_side_effects=True, vmem_limit_bytes=VMEM_LIMIT
        ),
        name="collect",
    )(data, start, steering)


SLOTS = 8


def project_kernel(basis_ref, proj_ref, basis_v, out_v, in_sem, out_sem):
    nb, _, width, m = basis_ref.shape
    step_rows = out_v.shape[1]
    per = m // step_rows

    def load(b):
        return pltpu.make_async_copy(basis_ref.at[b], basis_v.at[b], in_sem.at[b])

    def put(b, r):
        slot = lax.rem(b * per + r, SLOTS)
        return pltpu.make_async_copy(
            out_v.at[slot], proj_ref.at[b, pl.ds(r * step_rows, step_rows)], out_sem.at[slot]
        )

    def fetch(b, c):
        load(b).start()
        return c

    lax.fori_loop(0, nb, fetch, 0)

    def one(b, c):
        load(b).wait()
        low = basis_v[b, 0]
        tail = basis_v[b, 1]
        left = jnp.concatenate([low, tail, low], axis=0)
        right = jnp.concatenate([low, low, tail], axis=0)
        for r in range(per):

            @pl.when(b * per + r >= SLOTS)
            def _():
                put(b, r).wait()

            slot = lax.rem(b * per + r, SLOTS)
            out_v[slot] = dot(left[:, r * step_rows : (r + 1) * step_rows], right, 0, 0)
            put(b, r).start()
        return c

    lax.fori_loop(0, nb, one, 0)

    def drain(t, c):
        put(t // per, lax.rem(t, per)).wait()
        return c

    lax.fori_loop(max(nb * per - SLOTS, 0), nb * per, drain, 0)


def project(basis):
    nb, _, width, m = basis.shape
    step_rows = m // 4
    return pl.pallas_call(
        project_kernel,
        out_shape=jax.ShapeDtypeStruct((nb, m, m), F32),
        in_specs=[pl.BlockSpec(memory_space=pl.ANY)],
        out_specs=pl.BlockSpec(memory_space=pl.ANY),
        scratch_shapes=[
            pltpu.VMEM((nb, 2, width, m), BF16),
            pltpu.VMEM((SLOTS, step_rows, m), F32),
            pltpu.SemaphoreType.DMA((nb,)),
            pltpu.SemaphoreType.DMA((SLOTS,)),
        ],
        compiler_params=pltpu.CompilerParams(vmem_limit_bytes=VMEM_LIMIT),
        cost_estimate=pl.CostEstimate(
            flops=nb * m * m * width * 6, bytes_accessed=nb * m * m * 4, transcendentals=0
        ),
        name="project",
    )(basis)


def on_device(n, inner, data, steering, start):
    bins, rows, m = data.shape
    basis, noise = collect(data, start.transpose(0, 2, 1), steering, n, inner)
    held = lax.all_to_all(jnp.broadcast_to(noise, (n, noise.shape[1])), BOTH, 0, 0)
    projector = project(basis)
    spectrum = float(bins * m) / jnp.sum(held, axis=0)
    return (projector, spectrum)


def solution(mesh):
    P = jax.sharding.PartitionSpec
    inner = mesh.shape["bin"]
    n = mesh.shape["snap"] * inner
    return jax.shard_map(
        functools.partial(on_device, n, inner),
        mesh=mesh,
        in_specs=(P(None, BOTH, None), P(BOTH, None, None), P(BOTH, None, None)),
        out_specs=(P(BOTH, None, None), P()),
        check_vma=False,
    )
```

time: 108 us -> 98.7 us (0.914)
  Pallas kernels: 106 us -> 82.1 us
  starting transfers between devices: 0 us -> 13.3 us
    pallas_call x3 -> x2, Pallas kernels: 106 us -> 82.1 us  [the longest x1 69.6 us: collect(): pl.pallas_call(functools.partial(collect_kernel, n, inner), out_shape=(ja...]
    all_to_all x0 -> x1, starting transfers between devices: none -> 13.3 us  [on_device(): lax.all_to_all(jnp.broadcast_to(noise, (n, noise.shape[1])), BOTH, 0, 0)]
    broadcast_in_dim x0 -> x1, local copies, waits for them, and re-layouts: none -> 1.57 us  [on_device(): jnp.broadcast_to(noise, (n, noise.shape[1]))]
    unnamed x1 -> x0, local copies, waits for them, and re-layouts: 1.3 us -> none
  transfers between devices with their start and end apart: 0 -> 1, of which waited for: 0 -> 0; matrix products, arithmetic and copies ran while one was open for 0% -> 0% of each run, Pallas kernels for 0% -> 13%
where the time goes in v1:
time: 98.7 us; the launch traced here: 98.4 us
  Pallas kernels  82.1 us (83%)
  starting transfers between devices  13.3 us (13%)
  local copies, waits for them, and re-layouts  1.57 us (2%)
    pallas_call x1, Pallas kernels, collect(): pl.pallas_call(functools.partial(collect_kernel, n, inner), out_shape=(ja...  69.6 us
    all_to_all x1, starting transfers between devices, on_device(): lax.all_to_all(jnp.broadcast_to(noise, (n, noise.shape[1])), BOTH, 0, 0)  13.3 us
    pallas_call x1, Pallas kernels, project(): pl.pallas_call(project_kernel, out_shape=jax.ShapeDtypeStruct((nb, m, m),...  12.5 us
  transfers between devices with their start and end apart: 1, of which 0 were waited for; matrix products, arithmetic and copies ran while one was open for 0% of the time, Pallas kernels for 13%

profile of v1, /device:TPU:0, one launch (start us, length us, event | category | flops | bytes accessed | tf_op | source)
XLA Modules:
  0.0 98.4 jit_solution(13159506379857980953)
XLA Ops:
  0.6 69.6 %collect.1 = (bf16[8,2,64,1024]{3,2,1,0:T(8,128)(2,1)}, f32[1,2048]{1,0:T(1,128)}) custom-call(bf16[256,4,1024]{2,1,0:T(4,128)(2,1)} %data_ref.1, f32[8,64,1024]{2,1,0:T(8,128)} %bitcast.2, bf16[8,1024,2048]{2,1,0:T(8,128)(2,1)} %steer_ref.1), custom_call_target="tpu_custom_call" | custom-call | tf_op jit(solution)/shard_map/collect/pallas_call | solution.py:227
  70.2 1.6 %broadcast_in_dim.2 = f32[32,1,2048]{2,1,0:T(1,128)} broadcast(f32[2048]{0:T(1024)} %bitcast.3), dimensions={2} | broadcast | bytes 270336 | tf_op jit(solution)/shard_map/broadcast_in_dim | solution.py:335
  71.8 13.3 %all-to-all-start = ((f32[32,1,2048]{2,1,0:T(1,128)}), f32[32,1,2048]{2,1,0:T(1,128)S(1)}, u32[]{:S(2)}, u32[]{:S(2)}) async-start(f32[32,1,2048]{2,1,0:T(1,128)} %broadcast_in_dim.2), calls=%async_computation | async-start | bytes 524288 | tf_op jit(solution)/shard_map/all_to_all | solution.py:335
  85.1 12.5 %project.1 = f32[8,1024,1024]{2,1,0:T(8,128)} custom-call(bf16[8,2,64,1024]{3,2,1,0:T(8,128)(2,1)} %get-tuple-element.4.basis_ref), custom_call_target="tpu_custom_call" | custom-call | flops 3221225472 | bytes 33554432 | tf_op jit(solution)/shard_map/project/pallas_call | solution.py:313
  97.6 0.0 all-to-all-done
  97.6 0.2 reduce_sum.9
  97.8 0.6 broadcast_divide_fusion
Async XLA Ops:
  71.8 25.8 %all-to-all-start = ((f32[32,1,2048]{2,1,0:T(1,128)}), f32[32,1,2048]{2,1,0:T(1,128)S(1)}, u32[]{:S(2)}, u32[]{:S(2)}) async-start(f32[32,1,2048]{2,1,0:T(1,128)} %broadcast_in_dim.2), calls=%async_computation | async-start | bytes 524288 | tf_op jit(solution)/shard_map/all_to_all | solution.py:335

commit v2 on v1

--- a/solution.py
+++ b/solution.py
@@ -7,6 +7,7 @@
 from jax.experimental.pallas import tpu as pltpu
 
 ITERS = 3
+PIVOTS = 16
 F32 = jnp.float32
 BF16 = jnp.bfloat16
 MESH = pl.DeviceIdType.MESH
@@ -56,48 +57,56 @@
     return p[:, :c] + (p[:, c : 2 * c] + p[:, 2 * c :])
 
 
-def inverse_factors(grams):
-    size = grams[0].shape[0]
-    eye = (
-        lax.broadcasted_iota(jnp.int32, (size, size), 0)
-        == lax.broadcasted_iota(jnp.int32, (size, size), 1)
-    ).astype(F32)
-    rest = [jnp.concatenate([g, eye], axis=1) for g in grams]
+def inverse_factors(ga, gb):
+    size = ga.shape[0]
     wide = 2 * size
-    sub = lax.broadcasted_iota(jnp.int32, (8, wide), 0)
-    lane = lax.broadcasted_iota(jnp.int32, (8, size), 1)
-    done = [[] for _ in grams]
-    for t in range(size // 8):
-        tiles = [a[8 * t : 8 * t + 8] for a in rest]
-        cols = [
-            [jnp.broadcast_to(a[:, 8 * t + j : 8 * t + j + 1], (8, wide)) for j in range(8)]
-            for a in tiles
+    shape = (size, wide)
+    col = lax.broadcasted_iota(jnp.int32, shape, 1)
+    col = jnp.where(col >= size, col - size, col)
+    both = jnp.concatenate([ga, gb], axis=1)
+    unit = (col == lax.broadcasted_iota(jnp.int32, shape, 0)).astype(F32)
+    sub = lax.broadcasted_iota(jnp.int32, (PIVOTS, wide), 0)
+    lane = lax.broadcasted_iota(jnp.int32, (PIVOTS, wide), 1)
+    first = lane < size
+    lane = jnp.where(first, lane, lane - size)
+    pick = lax.broadcasted_iota(jnp.int32, (size, 2 * wide), 1)
+    pick = jnp.where(pick >= wide, pick - wide, pick) < size
+    done = []
+    for t in range(0, size, PIVOTS):
+        g = both[t : t + PIVOTS]
+        u = unit[t : t + PIVOTS]
+        c = [
+            jnp.where(
+                first,
+                jnp.broadcast_to(g[:, k : k + 1], (PIVOTS, wide)),
+                jnp.broadcast_to(g[:, size + k : size + k + 1], (PIVOTS, wide)),
+            )
+            for k in range(t, t + PIVOTS)
         ]
-        invs = [jnp.zeros((8, wide), F32) for _ in tiles]
-        for j in range(8):
-            for i in range(len(tiles)):
-                c = cols[i]
-                inv = 1.0 / c[j][j : j + 1]
-                below = jnp.where(sub > j, c[j], 0.0)
-                tiles[i] = tiles[i] - below * (tiles[i][j : j + 1] * inv)
-                for k in range(j + 1, 8):
-                    c[k] = c[k] - below * (c[k][j : j + 1] * inv)
-                invs[i] = jnp.where(sub == j, inv, invs[i])
-        for i in range(len(tiles)):
-            done[i].append(tiles[i] * jnp.sqrt(invs[i]))
-            if 8 * t + 8 < size:
-                scaled = (tiles[i] * invs[i])[:, :size]
-                h, m, l = split(jnp.where(lane >= 8 * t + 8, scaled, 0.0))
-                rh, rm, rl = split(tiles[i])
-                rest[i] = rest[i] - dot(
-                    stack([l, h, m, m, h, h], 0), stack([rh, rl, rm, rh, rm, rh], 0), 0, 0
-                )
-    return [jnp.concatenate(d, axis=0)[:, size:] for d in done]
+        invs = jnp.zeros((PIVOTS, wide), F32)
+        for j in range(PIVOTS):
+            inv = 1.0 / c[j][j : j + 1]
+            below = jnp.where(sub > j, c[j], 0.0)
+            g = g - below * (g[j : j + 1] * inv)
+            u = u - below * (u[j : j + 1] * inv)
+            for k in range(j + 1, PIVOTS):
+                c[k] = c[k] - below * (c[k][j : j + 1] * inv)
+            invs = jnp.where(sub == j, inv, invs)
+        done.append(u * jnp.sqrt(invs))
+        if t + PIVOTS < size:
+            h, m, l = split(jnp.where(lane >= t + PIVOTS, g * invs, 0.0))
+            rh, rm, rl = split(jnp.concatenate([g, u], axis=1))
+            d = dot(stack([l, h, m, m, h, h], 0), stack([rh, rl, rm, rh, rm, rh], 0), 0, 0)
+            d = jnp.where(pick, d[:size], d[size:])
+            both = both - d[:, :wide]
+            unit = unit - d[:, wide:]
+    f = jnp.concatenate(done, axis=0)
+    return f[:, :size], f[:, size:]
 
 
 def collect_kernel(
     n, inner, data_ref, start_ref, steer_ref, basis_ref, noise_ref,
-    x_v, start_v, steer_v, flat_v, s_v, v_v, basis_v, power_v,
+    x_v, start_v, steer_v, flat_v, s_v, v_v, basis_v, power_v, total_v,
     send_sem, recv_sem, own_sem, start_sem, steer_sem, basis_sem,
 ):
     nb, _, rows, m = x_v.shape
@@ -146,7 +155,8 @@
 
         return lax.fori_loop(1, n, one, c)
 
-    lax.fori_loop(0, groups, post, 0)
+    lead = min(2, groups)
+    lax.fori_loop(0, lead, post, 0)
 
     def arrived(p, sem):
         block = x_v.at[pl.ds(p * group, group), pl.ds(1, n - 1)]
@@ -166,12 +176,17 @@
         return c
 
     lax.fori_loop(0, nb, energies, 0)
-    noise_ref[...] = jnp.sum(power_v[...], axis=0, keepdims=True)
+    total_v[...] = jnp.sum(power_v[...], axis=0, keepdims=True)
     own.wait()
     first.wait()
 
     def process(p, c):
         arrived(p, recv_sem)
+
+        @pl.when(p + lead < groups)
+        def _():
+            post(p + lead, 0)
+
         for i in range(group):
             b = p * group + i
             x = x_v[b].reshape(kk, m)
@@ -188,7 +203,7 @@
                 w = fold_rows(fold_lanes(dot(vs, s_v[i], 1, 0)))
                 grams.append(fold_lanes(fold_rows(dot(stack(split(w), 0), vs, 1, 1))))
                 kept.append(jnp.where(last, v, w * (1.0 / kk)))
-            for i, factor in enumerate(inverse_factors(grams)):
+            for i, factor in zip(range(group), inverse_factors(grams[0], grams[-1])):
                 q = dot(stack(split(factor), 0), stack(split(kept[i]), 1), 1, 0)
                 v_v[i] = fold_rows(fold_lanes(q))
             return cc
@@ -202,11 +217,12 @@
             basis_v[b, 1] = (basis - low.astype(F32)).astype(BF16)
             for q in range(0, g, lanes):
                 along = dot(low, steer_v[b, :, q : q + lanes], 1, 0)
-                noise_ref[:, q : q + lanes] -= jnp.sum(along * along, axis=0, keepdims=True)
+                total_v[:, q : q + lanes] -= jnp.sum(along * along, axis=0, keepdims=True)
         put(p).start()
         return c
 
     lax.fori_loop(0, groups, process, 0)
+    noise_ref[...] = jnp.broadcast_to(total_v[...][None], noise_ref.shape)
 
     def close(p, c):
         arrived(p, send_sem)
@@ -228,7 +244,7 @@
         functools.partial(collect_kernel, n, inner),
         out_shape=(
             jax.ShapeDtypeStruct((nb, 2, width, m), BF16),
-            jax.ShapeDtypeStruct((1, g), F32),
+            jax.ShapeDtypeStruct((n, 1, g), F32),
         ),
         in_specs=[pl.BlockSpec(memory_space=pl.ANY)] * 3,
         out_specs=(
@@ -244,6 +260,7 @@
             pltpu.VMEM((group, width, kk), F32),
             pltpu.VMEM((nb, 2, width, m), BF16),
             pltpu.VMEM((8, g), F32),
+            pltpu.VMEM((1, g), F32),
             pltpu.SemaphoreType.DMA((groups,)),
             pltpu.SemaphoreType.DMA((groups,)),
             pltpu.SemaphoreType.DMA,
@@ -332,9 +349,9 @@
 def on_device(n, inner, data, steering, start):
     bins, rows, m = data.shape
     basis, noise = collect(data, start.transpose(0, 2, 1), steering, n, inner)
-    held = lax.all_to_all(jnp.broadcast_to(noise, (n, noise.shape[1])), BOTH, 0, 0)
+    held = lax.all_to_all(noise, BOTH, 0, 0)
     projector = project(basis)
-    spectrum = float(bins * m) / jnp.sum(held, axis=0)
+    spectrum = float(bins * m) / jnp.sum(held, axis=(0, 1))
     return (projector, spectrum)
 
 

time: 98.7 us -> 88.7 us (0.90)
  Pallas kernels: 82.1 us -> 76.7 us
  starting transfers between devices: 13.3 us -> 10.4 us
  local copies, waits for them, and re-layouts: 1.57 us -> 0 us
    pallas_call x1, Pallas kernels: 69.6 us -> 64.2 us  [collect(): pl.pallas_call(functools.partial(collect_kernel, n, inner), out_shape=(ja...]
    all_to_all x1, starting transfers between devices: 13.3 us -> 10.4 us  [on_device(): held = lax.all_to_all(noise, BOTH, 0, 0)]
    broadcast_in_dim x1 -> x0, local copies, waits for them, and re-layouts: 1.57 us -> none  [on_device(): jnp.broadcast_to(noise, (n, noise.shape[1]))]
  transfers between devices with their start and end apart: 1 -> 1, of which waited for: 0 -> 0; matrix products, arithmetic and copies ran while one was open for 0% -> 0% of each run, Pallas kernels for 13% -> 14%
where the time goes in v2:
time: 88.7 us; the launch traced here: 88.5 us
  Pallas kernels  76.7 us (86%)
  starting transfers between devices  10.4 us (12%)
    pallas_call x1, Pallas kernels, collect(): pl.pallas_call(functools.partial(collect_kernel, n, inner), out_shape=(ja...  64.2 us
    pallas_call x1, Pallas kernels, project(): pl.pallas_call(project_kernel, out_shape=jax.ShapeDtypeStruct((nb, m, m),...  12.5 us
    all_to_all x1, starting transfers between devices, on_device(): held = lax.all_to_all(noise, BOTH, 0, 0)  10.4 us
  transfers between devices with their start and end apart: 1, of which 0 were waited for; matrix products, arithmetic and copies ran while one was open for 0% of the time, Pallas kernels for 14%

profile of v2, /device:TPU:0, one launch (start us, length us, event | category | flops | bytes accessed | tf_op | source)
XLA Modules:
  0.0 88.5 jit_solution(2350179352804803510)
XLA Ops:
  0.6 64.2 %collect.1 = (bf16[8,2,64,1024]{3,2,1,0:T(8,128)(2,1)}, f32[32,1,2048]{2,1,0:T(1,128)}) custom-call(bf16[256,4,1024]{2,1,0:T(4,128)(2,1)} %data_ref.1, f32[8,64,1024]{2,1,0:T(8,128)} %bitcast.1, bf16[8,1024,2048]{2,1,0:T(8,128)(2,1)} %steer_ref.1), custom_call_target="tpu_custom_call" | custom-call | tf_op jit(solution)/shard_map/collect/pallas_call | solution.py:243
  64.8 10.4 %all-to-all-start = ((f32[32,1,2048]{2,1,0:T(1,128)}), f32[32,1,2048]{2,1,0:T(1,128)S(1)}, u32[]{:S(2)}, u32[]{:S(2)}) async-start(f32[32,1,2048]{2,1,0:T(1,128)} %get-tuple-element.5), calls=%async_computation | async-start | bytes 524288 | tf_op jit(solution)/shard_map/all_to_all | solution.py:352
  75.2 12.5 %project.1 = f32[8,1024,1024]{2,1,0:T(8,128)} custom-call(bf16[8,2,64,1024]{3,2,1,0:T(8,128)(2,1)} %get-tuple-element.4.basis_ref), custom_call_target="tpu_custom_call" | custom-call | flops 3221225472 | bytes 33554432 | tf_op jit(solution)/shard_map/project/pallas_call | solution.py:330
  87.7 0.0 all-to-all-done
  87.7 0.2 reduce_sum.9
  87.9 0.6 broadcast_divide_fusion
Async XLA Ops:
  64.8 22.9 %all-to-all-start = ((f32[32,1,2048]{2,1,0:T(1,128)}), f32[32,1,2048]{2,1,0:T(1,128)S(1)}, u32[]{:S(2)}, u32[]{:S(2)}) async-start(f32[32,1,2048]{2,1,0:T(1,128)} %get-tuple-element.5), calls=%async_computation | async-start | bytes 524288 | tf_op jit(solution)/shard_map/all_to_all | solution.py:352

commit v3 on v2

--- a/solution.py
+++ b/solution.py
@@ -106,7 +106,7 @@
 
 def collect_kernel(
     n, inner, data_ref, start_ref, steer_ref, basis_ref, noise_ref,
-    x_v, start_v, steer_v, flat_v, s_v, v_v, basis_v, power_v, total_v,
+    x_v, start_v, steer_v, flat_v, s_v, v_v, basis_v, power_v, total_v, parts_v,
     send_sem, recv_sem, own_sem, start_sem, steer_sem, basis_sem,
 ):
     nb, _, rows, m = x_v.shape
@@ -180,6 +180,12 @@
     own.wait()
     first.wait()
 
+    def cut(b, c):
+        parts_v[b] = stack(split(start_v[b]), 0)
+        return c
+
+    lax.fori_loop(0, nb, cut, 0)
+
     def process(p, c):
         arrived(p, recv_sem)
 
@@ -192,7 +198,7 @@
             x = x_v[b].reshape(kk, m)
             flat_v[i] = x
             s_v[i] = stack(split(dot(x, x, 1, 1)), 1)
-            v_v[i] = fold_rows(dot(stack(split(start_v[b]), 0), x, 1, 1))
+            v_v[i] = fold_rows(dot(parts_v[b], x, 1, 1))
 
         def step(it, cc):
             last = it == ITERS - 1
@@ -261,6 +267,7 @@
             pltpu.VMEM((nb, 2, width, m), BF16),
             pltpu.VMEM((8, g), F32),
             pltpu.VMEM((1, g), F32),
+            pltpu.VMEM((nb, 3 * width, m), BF16),
             pltpu.SemaphoreType.DMA((groups,)),
             pltpu.SemaphoreType.DMA((groups,)),
             pltpu.SemaphoreType.DMA,

time: 88.7 us -> 88.7 us (level)
  no operation moved by 1% of the time
where the time goes in v3:
time: 88.7 us; the launch traced here: 88.5 us
  Pallas kernels  76.7 us (86%)
  starting transfers between devices  10.3 us (12%)
    pallas_call x1, Pallas kernels, collect(): pl.pallas_call(functools.partial(collect_kernel, n, inner), out_shape=(ja...  64.2 us
    pallas_call x1, Pallas kernels, project(): pl.pallas_call(project_kernel, out_shape=jax.ShapeDtypeStruct((nb, m, m),...  12.5 us
    all_to_all x1, starting transfers between devices, on_device(): held = lax.all_to_all(noise, BOTH, 0, 0)  10.3 us
  transfers between devices with their start and end apart: 1, of which 0 were waited for; matrix products, arithmetic and copies ran while one was open for 0% of the time, Pallas kernels for 14%

profile of v3, /device:TPU:0, one launch (start us, length us, event | category | flops | bytes accessed | tf_op | source)
XLA Modules:
  0.0 88.5 jit_solution(1079514933702654534)
XLA Ops:
  0.6 64.2 %collect.1 = (bf16[8,2,64,1024]{3,2,1,0:T(8,128)(2,1)}, f32[32,1,2048]{2,1,0:T(1,128)}) custom-call(bf16[256,4,1024]{2,1,0:T(4,128)(2,1)} %data_ref.1, f32[8,64,1024]{2,1,0:T(8,128)} %bitcast.1, bf16[8,1024,2048]{2,1,0:T(8,128)(2,1)} %steer_ref.1), custom_call_target="tpu_custom_call" | custom-call | tf_op jit(solution)/shard_map/collect/pallas_call | solution.py:249
  64.8 10.3 %all-to-all-start = ((f32[32,1,2048]{2,1,0:T(1,128)}), f32[32,1,2048]{2,1,0:T(1,128)S(1)}, u32[]{:S(2)}, u32[]{:S(2)}) async-start(f32[32,1,2048]{2,1,0:T(1,128)} %get-tuple-element.5), calls=%async_computation | async-start | bytes 524288 | tf_op jit(solution)/shard_map/all_to_all | solution.py:359
  75.2 12.5 %project.1 = f32[8,1024,1024]{2,1,0:T(8,128)} custom-call(bf16[8,2,64,1024]{3,2,1,0:T(8,128)(2,1)} %get-tuple-element.4.basis_ref), custom_call_target="tpu_custom_call" | custom-call | flops 3221225472 | bytes 33554432 | tf_op jit(solution)/shard_map/project/pallas_call | solution.py:337
  87.7 0.0 all-to-all-done
  87.7 0.2 reduce_sum.9
  87.9 0.6 broadcast_divide_fusion
Async XLA Ops:
  64.8 22.9 %all-to-all-start = ((f32[32,1,2048]{2,1,0:T(1,128)}), f32[32,1,2048]{2,1,0:T(1,128)S(1)}, u32[]{:S(2)}, u32[]{:S(2)}) async-start(f32[32,1,2048]{2,1,0:T(1,128)} %get-tuple-element.5), calls=%async_computation | async-start | bytes 524288 | tf_op jit(solution)/shard_map/all_to_all | solution.py:359
